TPU v7x, 32 devices: a whole 2x2x4 slice. The times are simulated.
32 devices in a mesh: rows: 8 (over y, x, core), hub: 4 (over z).
Axes of the slice: x: 2, y: 2, z: 4, core: 2. Of those that a mesh axis runs over, the one named last changes fastest.
Arguments:
- tail_blocks: float32 [2304, 128, 128], P(('rows', 'hub')), may hold values from -0.21875 to 0.21875
- tail_row: int32 [2304], P(('rows', 'hub')), may hold values from 0 to 15
- tail_owner: int32 [2304, 1], P(('rows', 'hub')), may hold values from 0 to 7; in each aligned block of 72 rows (0 to 71, 72 to 143, ...) at most 27 rows name the same one
- tail_slot: int32 [2304], P(('rows', 'hub')), may hold values from 0 to 63
- hub_blocks: float32 [768, 128, 128], P(('rows', 'hub')), may hold values from -0.21875 to 0.21875
- hub_row: int32 [768], P(('rows', 'hub')), may hold values from 0 to 15
- hub_col: int32 [768], P(('rows', 'hub')), may hold values from 0 to 127
- x_tail: float32 [2048, 128], P(('rows', 'hub')), may hold values from 0 to 0.5
- cost_tail: float32 [2048, 128], P(('rows', 'hub')), may hold values from -6 to 6
- upper_tail: float32 [2048, 128], P(('rows', 'hub')), may hold values from 0.5 to 2
- x_hub: float32 [128, 128], P('hub'), may hold values from 0 to 0.5
- cost_hub: float32 [128, 128], P('hub'), may hold values from -6 to 6
- upper_hub: float32 [128, 128], P('hub'), may hold values from 0.5 to 2
- duals: float32 [512, 128], P(('rows', 'hub')), may hold values from 0 to 1
- demand: float32 [512, 128], P(('rows', 'hub')), may hold values from -6 to 6
Outputs:
- x_tail_out: float32 [2048, 128], P(('rows', 'hub'))
- x_hub_out: float32 [128, 128], P('hub')
- duals_out: float32 [512, 128], P(('rows', 'hub'))
Inputs may be any that keep to these rules, and one draw needn't show every extreme that they name: `tail_owner`: among the blocks of one device no owner is named more than 27 times; on some device one owner is named exactly 27 times.
All inputs are finite; a program needn't handle non-finite values.
Results may differ from a plain program's by a relative error of at most 0.0001.
Values sent between devices are 32-bit elements; how exact they have to be, the bound alone decides.
No kernel may reach another device: no remote copies, remote signals or barrier semaphores. Data moves between devices by JAX's collectives and lax.ppermute only.
A program may use at most 64 MiB of HBM per device.

v0:
```python
import jax
import jax.numpy as jnp
from jax import lax
from jax.sharding import PartitionSpec as P

ITERS = 3
primal_step = 0.25
dual_step = 0.25


def on_device(
    tail_blocks,
    tail_row,
    tail_owner,
    tail_slot,
    hub_blocks,
    hub_row,
    hub_col,
    x_tail,
    cost_tail,
    upper_tail,
    x_hub,
    cost_hub,
    upper_hub,
    duals,
    demand,
):
    highest = lax.Precision.HIGHEST
    row_devs = lax.axis_size("rows")
    hub_devs = lax.axis_size("hub")
    tail_count = tail_blocks.shape[0]
    col_blocks = x_tail.shape[0]
    row_blocks = duals.shape[0]
    hub_share = x_hub.shape[0]
    hub_total = hub_share * hub_devs
    width = x_tail.shape[1]
    capacity = max(2, 3 * tail_count // row_devs)
    owners = tail_owner[:, 0]
    hits = (owners[:, None] == jnp.arange(row_devs, dtype=jnp.int32)[None, :]).astype(jnp.int32)
    within = jnp.sum(jnp.cumsum(hits, axis=0) * hits, axis=1) - 1
    places = owners * capacity + within
    asked_slots = jnp.zeros((row_devs * capacity,), jnp.int32).at[places].set(tail_slot)
    requested = lax.all_to_all(
        asked_slots.reshape(row_devs, capacity), "rows", split_axis=0, concat_axis=0, tiled=True
    ).reshape(-1)
    collector = (jnp.arange(col_blocks, dtype=jnp.int32)[:, None] == requested[None, :]).astype(
        jnp.float32
    )
    tail_rowpick = (jnp.arange(row_blocks, dtype=jnp.int32)[:, None] == tail_row[None, :]).astype(
        jnp.float32
    )
    hub_rowpick = (jnp.arange(row_blocks, dtype=jnp.int32)[:, None] == hub_row[None, :]).astype(
        jnp.float32
    )
    hub_state = x_hub
    hub_pick = (jnp.arange(hub_total, dtype=jnp.int32)[:, None] == hub_col[None, :]).astype(
        jnp.float32
    )
    tail_state = x_tail
    for iteration in range(ITERS):
        tail_terms = jnp.einsum("bij,bi->bj", tail_blocks, duals[tail_row], precision=highest)
        outgoing = jnp.zeros((row_devs * capacity, width), jnp.float32).at[places].set(tail_terms)
        arrived = lax.all_to_all(
            outgoing.reshape(row_devs, capacity, width),
            "rows",
            split_axis=0,
            concat_axis=0,
            tiled=True,
        )
        tail_image = jnp.dot(
            collector,
            arrived.reshape(-1, width),
            precision=highest,
            preferred_element_type=jnp.float32,
        )
        tail_next = jnp.minimum(
            jnp.maximum(tail_state - primal_step * (cost_tail - tail_image), 0.0), upper_tail
        )
        tail_extra = 2.0 * tail_next - tail_state
        hub_terms = jnp.einsum("bij,bi->bj", hub_blocks, duals[hub_row], precision=highest)
        hub_partial = jnp.dot(
            hub_pick, hub_terms, precision=highest, preferred_element_type=jnp.float32
        )
        hub_sums = lax.psum_scatter(hub_partial, "hub", scatter_dimension=0, tiled=True)
        hub_sums = lax.psum(hub_sums, "rows")
        hub_next = jnp.minimum(
            jnp.maximum(hub_state - primal_step * (cost_hub - hub_sums), 0.0), upper_hub
        )
        hub_extra = 2.0 * hub_next - hub_state
        hub_full = lax.all_gather(hub_extra, "hub", axis=0, tiled=True)
        gathered = lax.all_gather(tail_extra, "rows", axis=0, tiled=True)
        tail_picked = gathered[owners * col_blocks + tail_slot]
        tail_product = jnp.einsum("bij,bj->bi", tail_blocks, tail_picked, precision=highest)
        hub_product = jnp.einsum("bij,bj->bi", hub_blocks, hub_full[hub_col], precision=highest)
        primal_image = jnp.dot(
            tail_rowpick, tail_product, precision=highest, preferred_element_type=jnp.float32
        )
        primal_image = primal_image + jnp.dot(
            hub_rowpick, hub_product, precision=highest, preferred_element_type=jnp.float32
        )
        duals = jnp.maximum(duals + dual_step * (demand - primal_image), 0.0)
        tail_state = tail_next
        hub_state = hub_next
    return (tail_state, hub_state, duals)


def solution(mesh):
    in_specs = (
        P(("rows", "hub"), None, None),
        P(("rows", "hub")),
        P(("rows", "hub"), None),
        P(("rows", "hub")),
        P(("rows", "hub"), None, None),
        P(("rows", "hub")),
        P(("rows", "hub")),
        P(("rows", "hub"), None),
        P(("rows", "hub"), None),
        P(("rows", "hub"), None),
        P("hub", None),
        P("hub", None),
        P("hub", None),
        P(("rows", "hub"), None),
        P(("rows", "hub"), None),
    )
    out_specs = (P(("rows", "hub"), None), P("hub", None), P(("rows", "hub"), None))
    return jax.shard_map(
        on_device, mesh=mesh, in_specs=in_specs, out_specs=out_specs, check_vma=False
    )
```

profile of v0, /device:TPU:0, one launch (start us, length us, event | category | flops | bytes accessed | tf_op | source)
XLA Modules:
  0.0 261.1 jit_solution(8980955782605521598)
XLA Ops:
  9.7 0.9 scatter_custom_fusion
  11.3 5.2 %all-to-all-start = ((s32[8,1,27]{2,1,0:T(1,128)}), s32[8,1,27]{2,1,0:T(1,128)S(1)}, u32[]{:S(2)}, u32[]{:S(2)}) async-start(s32[8,1,27]{2,1,0:T(1,128)} %all_to_all.15), calls=%async_computation | async-start | bytes 8192 | tf_op jit(solution)/shard_map/all_to_all | solution.py:43
  17.2 1.3 gather_fusion.2
  18.5 1.4 fusion.54
  19.9 1.5 fusion.26
  23.4 1.3 gather_fusion
  24.7 5.8 %fusion.52 = f32[72,1,128]{2,1,0:T(1,128)S(1)} fusion(f32[72,128,1]{1,2,0:T(1,128)S(1)} %bitcast.112, f32[72,128,128]{2,1,0:T(8,128)} %param.15), kind=kOutput, calls=%fused_computation.99 | convolution fusion | flops 14155776 | bytes 4792320 | tf_op jit(solution)/shard_map/bij,bi->bj/dot_general | solution.py:61
  32.0 4.2 %all-to-all-start.1 = ((f32[8,27,128]{2,1,0:T(8,128)}), f32[8,27,128]{2,1,0:T(8,128)S(1)}, u32[]{:S(2)}, u32[]{:S(2)}) async-start(f32[8,27,128]{2,1,0:T(8,128)} %reshape.42), calls=%async_computation.1 | async-start | bytes 262144 | tf_op jit(solution)/shard_map/all_to_all | solution.py:63
  37.4 4.2 %all-to-all-done.1 = f32[8,27,128]{2,1,0:T(8,128)S(1)} async-done(((f32[8,27,128]{2,1,0:T(8,128)}), f32[8,27,128]{2,1,0:T(8,128)S(1)}, u32[]{:S(2)}, u32[]{:S(2)}) %all-to-all-start.1) | async-done | bytes 110624 | tf_op jit(solution)/shard_map/all_to_all | solution.py:63
  41.9 8.4 %all_gather.18 = f32[512,128]{1,0:T(8,128)S(1)} all-gather(f32[64,128]{1,0:T(8,128)S(1)} %get-tuple-element.9), channel_id=1, replica_groups=mesh['rows'=8,'hub'=4] {'rows'}, dimensions={0}, use_global_device_ids=true | all-gather | bytes 294912 | tf_op jit(solution)/shard_map/all_gather | solution.py:91
  50.9 9.2 %fusion.53 = f32[72,1,128]{2,1,0:T(1,128)S(1)} fusion(f32[72,128,1]{1,2,0:T(1,128)S(1)} %bitcast.109, f32[72,128,128]{2,1,0:T(8,128)} %param.15), kind=kOutput, calls=%fused_computation.100 | convolution fusion | flops 14155776 | bytes 4792320 | tf_op jit(solution)/shard_map/bij,bj->bi/dot_general | solution.py:93
  60.2 23.7 %psum.21 = f32[32,128]{1,0:T(8,128)S(1)} all-reduce(f32[32,128]{1,0:T(8,128)} %reduce-scatter.4.cloned.1.call-done), channel_id=1, replica_groups=mesh['rows'=8,'hub'=4] {'rows'}, use_global_device_ids=true, to_apply=%region_5.6 | all-reduce | flops 4096 | bytes 32768 | tf_op jit(solution)/shard_map/psum | solution.py:85
  84.0 13.6 %all_gather.19 = f32[128,128]{1,0:T(8,128)S(1)} all-gather(f32[32,128]{1,0:T(8,128)S(1)} %get-tuple-element.7), channel_id=1, replica_groups=mesh['rows'=8,'hub'=4] {'hub'}, dimensions={0}, use_global_device_ids=true | all-gather | bytes 81920 | tf_op jit(solution)/shard_map/all_gather | solution.py:90
  98.1 2.5 fusion.55
  102.0 5.8 %fusion.56 = f32[72,1,128]{2,1,0:T(1,128)S(1)} fusion(f32[72,128,1]{1,2,0:T(1,128)S(1)} %bitcast.110, f32[72,128,128]{2,1,0:T(8,128)} %param.15), kind=kOutput, calls=%fused_computation.103 | convolution fusion | flops 14155776 | bytes 4792320 | tf_op jit(solution)/shard_map/bij,bi->bj/dot_general | solution.py:61
  109.2 3.4 %all-to-all-start.2 = ((f32[8,27,128]{2,1,0:T(8,128)}), f32[8,27,128]{2,1,0:T(8,128)S(1)}, u32[]{:S(2)}, u32[]{:S(2)}) async-start(f32[8,27,128]{2,1,0:T(8,128)} %reshape.44), calls=%async_computation.3 | async-start | bytes 262144 | tf_op jit(solution)/shard_map/all_to_all | solution.py:63
  112.7 1.4 fusion.58
  115.0 3.2 %all-to-all-done.2 = f32[8,27,128]{2,1,0:T(8,128)S(1)} async-done(((f32[8,27,128]{2,1,0:T(8,128)}), f32[8,27,128]{2,1,0:T(8,128)S(1)}, u32[]{:S(2)}, u32[]{:S(2)}) %all-to-all-start.2) | async-done | bytes 110624 | tf_op jit(solution)/shard_map/all_to_all | solution.py:63
  118.4 8.4 %all_gather.20 = f32[512,128]{1,0:T(8,128)S(1)} all-gather(f32[64,128]{1,0:T(8,128)S(1)} %get-tuple-element.11), channel_id=1, replica_groups=mesh['rows'=8,'hub'=4] {'rows'}, dimensions={0}, use_global_device_ids=true | all-gather | bytes 294912 | tf_op jit(solution)/shard_map/all_gather | solution.py:91
  127.3 9.2 %fusion.57 = f32[72,1,128]{2,1,0:T(1,128)S(1)} fusion(f32[72,128,1]{1,2,0:T(1,128)S(1)} %bitcast.111, f32[72,128,128]{2,1,0:T(8,128)} %param.15), kind=kOutput, calls=%fused_computation.104 | convolution fusion | flops 14155776 | bytes 4792320 | tf_op jit(solution)/shard_map/bij,bj->bi/dot_general | solution.py:93
  136.7 23.6 %psum.22 = f32[32,128]{1,0:T(8,128)S(1)} all-reduce(f32[32,128]{1,0:T(8,128)} %reduce-scatter.6.cloned.1.call-done), channel_id=1, replica_groups=mesh['rows'=8,'hub'=4] {'rows'}, use_global_device_ids=true, to_apply=%region_8.9 | all-reduce | flops 4096 | bytes 32768 | tf_op jit(solution)/shard_map/psum | solution.py:85
  160.3 13.4 %all_gather.21 = f32[128,128]{1,0:T(8,128)S(1)} all-gather(f32[32,128]{1,0:T(8,128)S(1)} %get-tuple-element.5), channel_id=1, replica_groups=mesh['rows'=8,'hub'=4] {'hub'}, dimensions={0}, use_global_device_ids=true | all-gather | bytes 81920 | tf_op jit(solution)/shard_map/all_gather | solution.py:90
  174.2 2.5 fusion.59
  178.1 5.8 %fusion.60 = f32[72,1,128]{2,1,0:T(1,128)S(1)} fusion(f32[72,128,1]{1,2,0:T(1,128)S(1)} %bitcast.107, f32[72,128,128]{2,1,0:T(8,128)} %param.15), kind=kOutput, calls=%fused_computation.107 | convolution fusion | flops 14155776 | bytes 4792320 | tf_op jit(solution)/shard_map/bij,bi->bj/dot_general | solution.py:61
  185.3 3.4 %all-to-all-start.3 = ((f32[8,27,128]{2,1,0:T(8,128)}), f32[8,27,128]{2,1,0:T(8,128)S(1)}, u32[]{:S(2)}, u32[]{:S(2)}) async-start(f32[8,27,128]{2,1,0:T(8,128)} %reshape.46), calls=%async_computation.5 | async-start | bytes 262144 | tf_op jit(solution)/shard_map/all_to_all | solution.py:63
  188.8 1.4 fusion.61
  191.0 3.2 %all-to-all-done.3 = f32[8,27,128]{2,1,0:T(8,128)S(1)} async-done(((f32[8,27,128]{2,1,0:T(8,128)}), f32[8,27,128]{2,1,0:T(8,128)S(1)}, u32[]{:S(2)}, u32[]{:S(2)}) %all-to-all-start.3) | async-done | bytes 110624 | tf_op jit(solution)/shard_map/all_to_all | solution.py:63
  195.1 8.3 %all_gather.22 = f32[512,128]{1,0:T(8,128)S(1)} all-gather(f32[64,128]{1,0:T(8,128)S(1)} %get-tuple-element.13), channel_id=1, replica_groups=mesh['rows'=8,'hub'=4] {'rows'}, dimensions={0}, use_global_device_ids=true | all-gather | bytes 294912 | tf_op jit(solution)/shard_map/all_gather | solution.py:91
  204.0 9.2 %fusion.62 = f32[72,1,128]{2,1,0:T(1,128)S(1)} fusion(f32[72,128,1]{1,2,0:T(1,128)S(1)} %bitcast.108, f32[72,128,128]{2,1,0:T(8,128)} %param.15), kind=kOutput, calls=%fused_computation.109 | convolution fusion | flops 14155776 | bytes 4792320 | tf_op jit(solution)/shard_map/bij,bj->bi/dot_general | solution.py:93
  213.3 23.6 %psum.23 = f32[32,128]{1,0:T(8,128)S(1)} all-reduce(f32[32,128]{1,0:T(8,128)} %reduce-scatter.8.cloned.1.call-done), channel_id=1, replica_groups=mesh['rows'=8,'hub'=4] {'rows'}, use_global_device_ids=true, to_apply=%region_11.12 | all-reduce | flops 4096 | bytes 32768 | tf_op jit(solution)/shard_map/psum | solution.py:85
  237.6 13.1 %all_gather.23 = f32[128,128]{1,0:T(8,128)S(1)} all-gather(f32[32,128]{1,0:T(8,128)S(1)} %get-tuple-element.3), channel_id=1, replica_groups=mesh['rows'=8,'hub'=4] {'hub'}, dimensions={0}, use_global_device_ids=true | all-gather | bytes 81920 | tf_op jit(solution)/shard_map/all_gather | solution.py:90
  251.2 2.5 fusion.63
  (83 shorter events, 22.4 us)
Async XLA Ops:
  7.2 11.3 %copy-start = (f32[24,128,128]{2,1,0:T(8,128)S(1)}, f32[24,128,128]{2,1,0:T(8,128)}, u32[]{:S(2)}) copy-start(f32[24,128,128]{2,1,0:T(8,128)} %param.19) | copy-start | bytes 4718596
  7.2 34.5 %copy-start.7 = (f32[64,128]{1,0:T(8,128)S(1)}, f32[64,128]{1,0:T(8,128)}, u32[]{:S(2)}) copy-start(f32[64,128]{1,0:T(8,128)} %param.22) | copy-start | bytes 98308
  7.2 34.5 %copy-start.3 = (f32[64,128]{1,0:T(8,128)S(1)}, f32[64,128]{1,0:T(8,128)}, u32[]{:S(2)}) copy-start(f32[64,128]{1,0:T(8,128)} %param.23) | copy-start | bytes 98308
  7.2 34.5 %copy-start.2 = (f32[64,128]{1,0:T(8,128)S(1)}, f32[64,128]{1,0:T(8,128)}, u32[]{:S(2)}) copy-start(f32[64,128]{1,0:T(8,128)} %param.24) | copy-start | bytes 98308
  11.3 20.7 %all-to-all-start = ((s32[8,1,27]{2,1,0:T(1,128)}), s32[8,1,27]{2,1,0:T(1,128)S(1)}, u32[]{:S(2)}, u32[]{:S(2)}) async-start(s32[8,1,27]{2,1,0:T(1,128)} %all_to_all.15), calls=%async_computation | async-start | bytes 8192 | tf_op jit(solution)/shard_map/all_to_all | solution.py:43
  16.5 43.7 %reduce-scatter.4.cloned.1.call-start = ((), (), s32[]{:S(2)}) async-start(), calls=%async_computation.7 | async-start | bytes 81920 | tf_op jit(solution)/shard_map/reduce_scatter | solution.py:84
  24.7 35.4 %copy-start.10 = (s32[72]{0:T(128)S(1)}, s32[72]{0:T(128)}, u32[]{:S(2)}) copy-start(s32[72]{0:T(128)} %param.16) | copy-start | bytes 868
  24.7 59.2 %copy-start.4 = (f32[32,128]{1,0:T(8,128)S(1)}, f32[32,128]{1,0:T(8,128)}, u32[]{:S(2)}) copy-start(f32[32,128]{1,0:T(8,128)} %param.27) | copy-start | bytes 49156
  24.7 59.2 %copy-start.5 = (f32[32,128]{1,0:T(8,128)S(1)}, f32[32,128]{1,0:T(8,128)}, u32[]{:S(2)}) copy-start(f32[32,128]{1,0:T(8,128)} %param.26) | copy-start | bytes 49156
  24.7 59.2 %copy-start.8 = (f32[32,128]{1,0:T(8,128)S(1)}, f32[32,128]{1,0:T(8,128)}, u32[]{:S(2)}) copy-start(f32[32,128]{1,0:T(8,128)} %param.25) | copy-start | bytes 49156
  30.5 70.1 %copy-start.1 = (f32[16,128]{1,0:T(8,128)S(1)}, f32[16,128]{1,0:T(8,128)}, u32[]{:S(2)}) copy-start(f32[16,128]{1,0:T(8,128)} %param.28) | copy-start | bytes 24580
  30.5 70.1 %copy-start.6 = (f32[16,128]{1,0:T(8,128)S(1)}, f32[16,128]{1,0:T(8,128)}, u32[]{:S(2)}) copy-start(f32[16,128]{1,0:T(8,128)} %param.29) | copy-start | bytes 24580
  30.5 70.2 %copy-start.11 = (s32[24]{0:T(128)S(1)}, s32[24]{0:T(128)}, u32[]{:S(2)}) copy-start(s32[24]{0:T(128)} %param.20) | copy-start | bytes 292
  32.0 9.7 %all-to-all-start.1 = ((f32[8,27,128]{2,1,0:T(8,128)}), f32[8,27,128]{2,1,0:T(8,128)S(1)}, u32[]{:S(2)}, u32[]{:S(2)}) async-start(f32[8,27,128]{2,1,0:T(8,128)} %reshape.42), calls=%async_computation.1 | async-start | bytes 262144 | tf_op jit(solution)/shard_map/all_to_all | solution.py:63
  60.2 53.9 %copy-start.9 = (s32[24]{0:T(128)S(1)}, s32[24]{0:T(128)}, u32[]{:S(2)}) copy-start(s32[24]{0:T(128)} %param.21) | copy-start | bytes 292
  109.2 8.9 %all-to-all-start.2 = ((f32[8,27,128]{2,1,0:T(8,128)}), f32[8,27,128]{2,1,0:T(8,128)S(1)}, u32[]{:S(2)}, u32[]{:S(2)}) async-start(f32[8,27,128]{2,1,0:T(8,128)} %reshape.44), calls=%async_computation.3 | async-start | bytes 262144 | tf_op jit(solution)/shard_map/all_to_all | solution.py:63
  112.7 24.0 %reduce-scatter.6.cloned.1.call-start = ((), (), s32[]{:S(2)}) async-start(), calls=%async_computation.8 | async-start | bytes 81920 | tf_op jit(solution)/shard_map/reduce_scatter | solution.py:84
  185.3 8.9 %all-to-all-start.3 = ((f32[8,27,128]{2,1,0:T(8,128)}), f32[8,27,128]{2,1,0:T(8,128)S(1)}, u32[]{:S(2)}, u32[]{:S(2)}) async-start(f32[8,27,128]{2,1,0:T(8,128)} %reshape.46), calls=%async_computation.5 | async-start | bytes 262144 | tf_op jit(solution)/shard_map/all_to_all | solution.py:63
  188.7 24.6 %reduce-scatter.8.cloned.1.call-start = ((), (), s32[]{:S(2)}) async-start(), calls=%async_computation.9 | async-start | bytes 81920 | tf_op jit(solution)/shard_map/reduce_scatter | solution.py:84
Sparse Core Ops, SparseCore 0:
  21.5 20.9 reduce-scatter.3
  115.7 20.7 reduce-scatter.5
  191.8 20.7 reduce-scatter.7
where the time goes:
time: 262 us; the launch traced here: 261 us
  blocking collectives  136 us (52%)
  matrix products  62.6 us (24%)
  starting transfers between devices  16.3 us (6%)
  local copies, waits for them, and re-layouts  15 us (6%)
  between operations  14 us (5%)
  waiting for transfers between devices  10.7 us (4%)
  other arithmetic  6.44 us (2%)
    psum x3, blocking collectives, on_device(): hub_sums = lax.psum(hub_sums, 'rows')  70.9 us
    all_gather x3, blocking collectives, on_device(): hub_full = lax.all_gather(hub_extra, 'hub', axis=0, tiled=True)  40.1 us
    dot_general x3, matrix products, on_device(): jnp.einsum('bij,bj->bi', tail_blocks, tail_picked, precision=highest)  27.6 us
    all_gather x3, blocking collectives, on_device(): gathered = lax.all_gather(tail_extra, 'rows', axis=0, tiled=True)  25 us
    dot_general x3, matrix products, on_device(): jnp.einsum('bij,bi->bj', tail_blocks, duals[tail_row], precision=highest)  17.4 us
    all_to_all x3, starting transfers between devices, on_device(): lax.all_to_all(outgoing.reshape(row_devs, capacity, width), 'rows', split...  11 us
    all_to_all x3, waiting for transfers between devices, on_device(): lax.all_to_all(outgoing.reshape(row_devs, capacity, width), 'rows', split...  10.6 us
    dot_general x3, matrix products, on_device(): jnp.einsum('bij,bj->bi', hub_blocks, hub_full[hub_col], precision=highest)  7.63 us
  transfers between devices with their start and end apart: 7, of which 3 were waited for; matrix products, arithmetic and copies ran while one was open for 20% of the time, Pallas kernels for 0%

commit v1 on v0

--- a/solution.py
+++ b/solution.py
@@ -82,7 +82,11 @@
             hub_pick, hub_terms, precision=highest, preferred_element_type=jnp.float32
         )
         hub_sums = lax.psum_scatter(hub_partial, "hub", scatter_dimension=0, tiled=True)
-        hub_sums = lax.psum(hub_sums, "rows")
+        devices, acc = (lax.axis_size("rows"), hub_sums)
+        for far in [1 << k for k in range(devices.bit_length() - 1)]:
+            pairs = [(i, i ^ far) for i in range(devices)]
+            acc = acc + lax.ppermute(acc, "rows", pairs)
+        hub_sums = acc
         hub_next = jnp.minimum(
             jnp.maximum(hub_state - primal_step * (cost_hub - hub_sums), 0.0), upper_hub
         )

time: 262 us -> 244 us (0.931)
  blocking collectives: 136 us -> 67.7 us
  waiting for transfers between devices: 10.7 us -> 51.9 us
  starting transfers between devices: 16.3 us -> 22.5 us
    psum x3 -> x0, blocking collectives: 70.9 us -> none  [on_device(): hub_sums = lax.psum(hub_sums, 'rows')]
    reduce_scatter x3, waiting for transfers between devices: 0.01 us -> 32.2 us  [on_device(): lax.psum_scatter(hub_partial, 'hub', scatter_dimension=0, tiled=True)]
    ppermute x0 -> x9, waiting for transfers between devices: none -> 9.15 us  [on_device(): acc = acc + lax.ppermute(acc, 'rows', pairs)]
    ppermute x0 -> x9, starting transfers between devices: none -> 6.28 us  [on_device(): acc = acc + lax.ppermute(acc, 'rows', pairs)]
    all_gather x3, blocking collectives: 25 us -> 27.8 us  [on_device(): gathered = lax.all_gather(tail_extra, 'rows', axis=0, tiled=True)]
  transfers between devices with their start and end apart: 7 -> 16, of which waited for: 3 -> 9; matrix products, arithmetic and copies ran while one was open for 20% -> 21% of each run, Pallas kernels for 0% -> 0%
where the time goes in v1:
time: 244 us; the launch traced here: 242 us
  blocking collectives  67.7 us (28%)
  matrix products  62.5 us (26%)
  waiting for transfers between devices  51.9 us (21%)
  starting transfers between devices  22.5 us (9%)
  local copies, waits for them, and re-layouts  15.1 us (6%)
  between operations  14.1 us (6%)
  other arithmetic  8.66 us (4%)
    all_gather x3, blocking collectives, on_device(): hub_full = lax.all_gather(hub_extra, 'hub', axis=0, tiled=True)  39.9 us
    reduce_scatter x3, waiting for transfers between devices, on_device(): lax.psum_scatter(hub_partial, 'hub', scatter_dimension=0, tiled=True)  32.2 us
    all_gather x3, blocking collectives, on_device(): gathered = lax.all_gather(tail_extra, 'rows', axis=0, tiled=True)  27.8 us
    dot_general x3, matrix products, on_device(): jnp.einsum('bij,bj->bi', tail_blocks, tail_picked, precision=highest)  27.6 us
    dot_general x3, matrix products, on_device(): jnp.einsum('bij,bi->bj', tail_blocks, duals[tail_row], precision=highest)  17.4 us
    all_to_all x3, starting transfers between devices, on_device(): lax.all_to_all(outgoing.reshape(row_devs, capacity, width), 'rows', split...  10.9 us
    all_to_all x3, waiting for transfers between devices, on_device(): lax.all_to_all(outgoing.reshape(row_devs, capacity, width), 'rows', split...  10.5 us
    ppermute x9, waiting for transfers between devices, on_device(): acc = acc + lax.ppermute(acc, 'rows', pairs)  9.15 us
  transfers between devices with their start and end apart: 16, of which 9 were waited for; matrix products, arithmetic and copies ran while one was open for 21% of the time, Pallas kernels for 0%

profile of v1, /device:TPU:0, one launch (start us, length us, event | category | flops | bytes accessed | tf_op | source)
XLA Modules:
  0.0 242.4 jit_solution(16396664872871633210)
XLA Ops:
  11.3 5.2 %all-to-all-start = ((s32[8,1,27]{2,1,0:T(1,128)}), s32[8,1,27]{2,1,0:T(1,128)S(1)}, u32[]{:S(2)}, u32[]{:S(2)}) async-start(s32[8,1,27]{2,1,0:T(1,128)} %all_to_all.15), calls=%async_computation | async-start | bytes 8192 | tf_op jit(solution)/shard_map/all_to_all | solution.py:43
  18.5 1.4 fusion.54
  19.9 1.5 fusion.26
  24.7 5.8 %fusion.52 = f32[72,1,128]{2,1,0:T(1,128)S(1)} fusion(f32[72,128,1]{1,2,0:T(1,128)S(1)} %bitcast.112, f32[72,128,128]{2,1,0:T(8,128)} %param.15), kind=kOutput, calls=%fused_computation.99 | convolution fusion | flops 14155776 | bytes 4792320 | tf_op jit(solution)/shard_map/bij,bi->bj/dot_general | solution.py:61
  32.0 4.2 %all-to-all-start.1 = ((f32[8,27,128]{2,1,0:T(8,128)}), f32[8,27,128]{2,1,0:T(8,128)S(1)}, u32[]{:S(2)}, u32[]{:S(2)}) async-start(f32[8,27,128]{2,1,0:T(8,128)} %reshape.42), calls=%async_computation.1 | async-start | bytes 262144 | tf_op jit(solution)/shard_map/all_to_all | solution.py:63
  37.4 4.2 %all-to-all-done.1 = f32[8,27,128]{2,1,0:T(8,128)S(1)} async-done(((f32[8,27,128]{2,1,0:T(8,128)}), f32[8,27,128]{2,1,0:T(8,128)S(1)}, u32[]{:S(2)}, u32[]{:S(2)}) %all-to-all-start.1) | async-done | bytes 110624 | tf_op jit(solution)/shard_map/all_to_all | solution.py:63
  42.5 9.2 %all_gather.18 = f32[512,128]{1,0:T(8,128)S(1)} all-gather(f32[64,128]{1,0:T(8,128)S(1)} %get-tuple-element.9), channel_id=1, replica_groups=mesh['rows'=8,'hub'=4] {'rows'}, dimensions={0}, use_global_device_ids=true | all-gather | bytes 294912 | tf_op jit(solution)/shard_map/all_gather | solution.py:95
  53.1 1.5 collective-permute-start.1
  54.6 9.2 %fusion.53 = f32[72,1,128]{2,1,0:T(1,128)S(1)} fusion(f32[72,128,1]{1,2,0:T(1,128)S(1)} %bitcast.108, f32[72,128,128]{2,1,0:T(8,128)} %param.15), kind=kOutput, calls=%fused_computation.100 | convolution fusion | flops 14155776 | bytes 4792320 | tf_op jit(solution)/shard_map/bij,bj->bi/dot_general | solution.py:97
  64.5 3.0 %collective-permute-done.2 = f32[32,128]{1,0:T(8,128)S(1)} collective-permute-done((f32[32,128]{1,0:T(8,128)S(1)}, f32[32,128]{1,0:T(8,128)S(1)}, u32[]{:S(2)}, u32[]{:S(2)}) %collective-permute-start.2) | collective-permute-done | bytes 16416 | tf_op jit(solution)/shard_map/ppermute | solution.py:88
  67.6 13.5 %all_gather.19 = f32[128,128]{1,0:T(8,128)S(1)} all-gather(f32[32,128]{1,0:T(8,128)S(1)} %get-tuple-element.7), channel_id=1, replica_groups=mesh['rows'=8,'hub'=4] {'hub'}, dimensions={0}, use_global_device_ids=true | all-gather | bytes 81920 | tf_op jit(solution)/shard_map/all_gather | solution.py:94
  81.7 2.5 %fusion.55 = f32[24,1,128]{2,1,0:T(1,128)S(1)} fusion(f32[24,128,1]{1,2,0:T(1,128)S(1)} %bitcast.117, f32[24,128,128]{2,1,0:T(8,128)S(1)} %copy-done), kind=kOutput, calls=%fused_computation.102 | convolution fusion | flops 4718592 | bytes 1597440 | tf_op jit(solution)/shard_map/bij,bj->bi/dot_general | solution.py:98
  85.5 5.8 %fusion.56 = f32[72,1,128]{2,1,0:T(1,128)S(1)} fusion(f32[72,128,1]{1,2,0:T(1,128)S(1)} %bitcast.111, f32[72,128,128]{2,1,0:T(8,128)} %param.15), kind=kOutput, calls=%fused_computation.103 | convolution fusion | flops 14155776 | bytes 4792320 | tf_op jit(solution)/shard_map/bij,bi->bj/dot_general | solution.py:61
  92.8 3.4 %all-to-all-start.2 = ((f32[8,27,128]{2,1,0:T(8,128)}), f32[8,27,128]{2,1,0:T(8,128)S(1)}, u32[]{:S(2)}, u32[]{:S(2)}) async-start(f32[8,27,128]{2,1,0:T(8,128)} %reshape.44), calls=%async_computation.3 | async-start | bytes 262144 | tf_op jit(solution)/shard_map/all_to_all | solution.py:63
  98.5 3.1 %all-to-all-done.2 = f32[8,27,128]{2,1,0:T(8,128)S(1)} async-done(((f32[8,27,128]{2,1,0:T(8,128)}), f32[8,27,128]{2,1,0:T(8,128)S(1)}, u32[]{:S(2)}, u32[]{:S(2)}) %all-to-all-start.2) | async-done | bytes 110624 | tf_op jit(solution)/shard_map/all_to_all | solution.py:63
  101.8 16.8 %reduce-scatter.6.cloned.1.call-done = f32[32,128]{1,0:T(8,128)} async-done(((f32[128,128]{1,0:T(8,128)}), f32[32,128]{1,0:T(8,128)}) %reduce-scatter.6.cloned.1.call-update) | async-done | bytes 16400 | tf_op jit(solution)/shard_map/reduce_scatter | solution.py:84
  118.6 9.3 %all_gather.20 = f32[512,128]{1,0:T(8,128)S(1)} all-gather(f32[64,128]{1,0:T(8,128)S(1)} %get-tuple-element.11), channel_id=1, replica_groups=mesh['rows'=8,'hub'=4] {'rows'}, dimensions={0}, use_global_device_ids=true | all-gather | bytes 294912 | tf_op jit(solution)/shard_map/all_gather | solution.py:95
  129.2 1.5 collective-permute-start.4
  130.7 9.2 %fusion.57 = f32[72,1,128]{2,1,0:T(1,128)S(1)} fusion(f32[72,128,1]{1,2,0:T(1,128)S(1)} %bitcast.109, f32[72,128,128]{2,1,0:T(8,128)} %param.15), kind=kOutput, calls=%fused_computation.104 | convolution fusion | flops 14155776 | bytes 4792320 | tf_op jit(solution)/shard_map/bij,bj->bi/dot_general | solution.py:97
  140.7 3.1 %collective-permute-done.5 = f32[32,128]{1,0:T(8,128)S(1)} collective-permute-done((f32[32,128]{1,0:T(8,128)S(1)}, f32[32,128]{1,0:T(8,128)S(1)}, u32[]{:S(2)}, u32[]{:S(2)}) %collective-permute-start.5) | collective-permute-done | bytes 16416 | tf_op jit(solution)/shard_map/ppermute | solution.py:88
  143.8 13.3 %all_gather.21 = f32[128,128]{1,0:T(8,128)S(1)} all-gather(f32[32,128]{1,0:T(8,128)S(1)} %get-tuple-element.5), channel_id=1, replica_groups=mesh['rows'=8,'hub'=4] {'hub'}, dimensions={0}, use_global_device_ids=true | all-gather | bytes 81920 | tf_op jit(solution)/shard_map/all_gather | solution.py:94
  157.7 2.5 %fusion.59 = f32[24,1,128]{2,1,0:T(1,128)S(1)} fusion(f32[24,128,1]{1,2,0:T(1,128)S(1)} %bitcast.119, f32[24,128,128]{2,1,0:T(8,128)S(1)} %copy-done), kind=kOutput, calls=%fused_computation.106 | convolution fusion | flops 4718592 | bytes 1597440 | tf_op jit(solution)/shard_map/bij,bj->bi/dot_general | solution.py:98
  161.5 5.8 %fusion.60 = f32[72,1,128]{2,1,0:T(1,128)S(1)} fusion(f32[72,128,1]{1,2,0:T(1,128)S(1)} %bitcast.110, f32[72,128,128]{2,1,0:T(8,128)} %param.15), kind=kOutput, calls=%fused_computation.107 | convolution fusion | flops 14155776 | bytes 4792320 | tf_op jit(solution)/shard_map/bij,bi->bj/dot_general | solution.py:61
  168.8 3.4 %all-to-all-start.3 = ((f32[8,27,128]{2,1,0:T(8,128)}), f32[8,27,128]{2,1,0:T(8,128)S(1)}, u32[]{:S(2)}, u32[]{:S(2)}) async-start(f32[8,27,128]{2,1,0:T(8,128)} %reshape.46), calls=%async_computation.5 | async-start | bytes 262144 | tf_op jit(solution)/shard_map/all_to_all | solution.py:63
  174.5 3.1 %all-to-all-done.3 = f32[8,27,128]{2,1,0:T(8,128)S(1)} async-done(((f32[8,27,128]{2,1,0:T(8,128)}), f32[8,27,128]{2,1,0:T(8,128)S(1)}, u32[]{:S(2)}, u32[]{:S(2)}) %all-to-all-start.3) | async-done | bytes 110624 | tf_op jit(solution)/shard_map/all_to_all | solution.py:63
  178.4 14.7 %reduce-scatter.8.cloned.1.call-done = f32[32,128]{1,0:T(8,128)} async-done(((f32[128,128]{1,0:T(8,128)}), f32[32,128]{1,0:T(8,128)}) %reduce-scatter.8.cloned.1.call-update) | async-done | bytes 16400 | tf_op jit(solution)/shard_map/reduce_scatter | solution.py:84
  193.2 9.3 %all_gather.22 = f32[512,128]{1,0:T(8,128)S(1)} all-gather(f32[64,128]{1,0:T(8,128)S(1)} %get-tuple-element.13), channel_id=1, replica_groups=mesh['rows'=8,'hub'=4] {'rows'}, dimensions={0}, use_global_device_ids=true | all-gather | bytes 294912 | tf_op jit(solution)/shard_map/all_gather | solution.py:95
  203.8 1.4 collective-permute-start.7
  205.2 9.2 %fusion.62 = f32[72,1,128]{2,1,0:T(1,128)S(1)} fusion(f32[72,128,1]{1,2,0:T(1,128)S(1)} %bitcast.107, f32[72,128,128]{2,1,0:T(8,128)} %param.15), kind=kOutput, calls=%fused_computation.109 | convolution fusion | flops 14155776 | bytes 4792320 | tf_op jit(solution)/shard_map/bij,bj->bi/dot_general | solution.py:97
  215.2 3.0 %collective-permute-done.8 = f32[32,128]{1,0:T(8,128)S(1)} collective-permute-done((f32[32,128]{1,0:T(8,128)S(1)}, f32[32,128]{1,0:T(8,128)S(1)}, u32[]{:S(2)}, u32[]{:S(2)}) %collective-permute-start.8) | collective-permute-done | bytes 16416 | tf_op jit(solution)/shard_map/ppermute | solution.py:88
  218.8 13.1 %all_gather.23 = f32[128,128]{1,0:T(8,128)S(1)} all-gather(f32[32,128]{1,0:T(8,128)S(1)} %get-tuple-element.3), channel_id=1, replica_groups=mesh['rows'=8,'hub'=4] {'hub'}, dimensions={0}, use_global_device_ids=true | all-gather | bytes 81920 | tf_op jit(solution)/shard_map/all_gather | solution.py:94
  232.5 2.5 %fusion.63 = f32[24,1,128]{2,1,0:T(1,128)S(1)} fusion(f32[24,128,1]{1,2,0:T(1,128)S(1)} %bitcast.115, f32[24,128,128]{2,1,0:T(8,128)S(1)} %copy-done), kind=kOutput, calls=%fused_computation.110 | convolution fusion | flops 4718592 | bytes 1597440 | tf_op jit(solution)/shard_map/bij,bj->bi/dot_general | solution.py:98
  (104 shorter events, 33.5 us)
Async XLA Ops:
  7.2 11.3 %copy-start = (f32[24,128,128]{2,1,0:T(8,128)S(1)}, f32[24,128,128]{2,1,0:T(8,128)}, u32[]{:S(2)}) copy-start(f32[24,128,128]{2,1,0:T(8,128)} %param.19) | copy-start | bytes 4718596
  7.2 34.5 %copy-start.7 = (f32[64,128]{1,0:T(8,128)S(1)}, f32[64,128]{1,0:T(8,128)}, u32[]{:S(2)}) copy-start(f32[64,128]{1,0:T(8,128)} %param.22) | copy-start | bytes 98308
  7.2 34.5 %copy-start.2 = (f32[64,128]{1,0:T(8,128)S(1)}, f32[64,128]{1,0:T(8,128)}, u32[]{:S(2)}) copy-start(f32[64,128]{1,0:T(8,128)} %param.24) | copy-start | bytes 98308
  7.2 34.5 %copy-start.3 = (f32[64,128]{1,0:T(8,128)S(1)}, f32[64,128]{1,0:T(8,128)}, u32[]{:S(2)}) copy-start(f32[64,128]{1,0:T(8,128)} %param.23) | copy-start | bytes 98308
  11.3 20.7 %all-to-all-start = ((s32[8,1,27]{2,1,0:T(1,128)}), s32[8,1,27]{2,1,0:T(1,128)S(1)}, u32[]{:S(2)}, u32[]{:S(2)}) async-start(s32[8,1,27]{2,1,0:T(1,128)} %all_to_all.15), calls=%async_computation | async-start | bytes 8192 | tf_op jit(solution)/shard_map/all_to_all | solution.py:43
  16.5 26.0 %reduce-scatter.4.cloned.1.call-start = ((), (), s32[]{:S(2)}) async-start(), calls=%async_computation.7 | async-start | bytes 81920 | tf_op jit(solution)/shard_map/reduce_scatter | solution.py:84
  24.7 39.7 %copy-start.10 = (s32[72]{0:T(128)S(1)}, s32[72]{0:T(128)}, u32[]{:S(2)}) copy-start(s32[72]{0:T(128)} %param.16) | copy-start | bytes 868
  24.7 42.9 %copy-start.4 = (f32[32,128]{1,0:T(8,128)S(1)}, f32[32,128]{1,0:T(8,128)}, u32[]{:S(2)}) copy-start(f32[32,128]{1,0:T(8,128)} %param.27) | copy-start | bytes 49156
  24.7 42.9 %copy-start.5 = (f32[32,128]{1,0:T(8,128)S(1)}, f32[32,128]{1,0:T(8,128)}, u32[]{:S(2)}) copy-start(f32[32,128]{1,0:T(8,128)} %param.26) | copy-start | bytes 49156
  24.7 42.9 %copy-start.8 = (f32[32,128]{1,0:T(8,128)S(1)}, f32[32,128]{1,0:T(8,128)}, u32[]{:S(2)}) copy-start(f32[32,128]{1,0:T(8,128)} %param.25) | copy-start | bytes 49156
  30.5 53.7 %copy-start.1 = (f32[16,128]{1,0:T(8,128)S(1)}, f32[16,128]{1,0:T(8,128)}, u32[]{:S(2)}) copy-start(f32[16,128]{1,0:T(8,128)} %param.28) | copy-start | bytes 24580
  30.5 53.7 %copy-start.6 = (f32[16,128]{1,0:T(8,128)S(1)}, f32[16,128]{1,0:T(8,128)}, u32[]{:S(2)}) copy-start(f32[16,128]{1,0:T(8,128)} %param.29) | copy-start | bytes 24580
  30.5 53.7 %copy-start.11 = (s32[24]{0:T(128)S(1)}, s32[24]{0:T(128)}, u32[]{:S(2)}) copy-start(s32[24]{0:T(128)} %param.20) | copy-start | bytes 292
  32.0 9.7 %all-to-all-start.1 = ((f32[8,27,128]{2,1,0:T(8,128)}), f32[8,27,128]{2,1,0:T(8,128)S(1)}, u32[]{:S(2)}, u32[]{:S(2)}) async-start(f32[8,27,128]{2,1,0:T(8,128)} %reshape.42), calls=%async_computation.1 | async-start | bytes 262144 | tf_op jit(solution)/shard_map/all_to_all | solution.py:63
  42.5 9.8 %collective-permute-start = (f32[32,128]{1,0:T(8,128)}, f32[32,128]{1,0:T(8,128)S(1)}, u32[]{:S(2)}, u32[]{:S(2)}) collective-permute-start(f32[32,128]{1,0:T(8,128)} %reduce-scatter.4.cloned.1.call-done), channel_id=1, source_target_pairs={{0,4},{4,0},{8,12},{12,8},{16,20},{20,16},{24,28},{28,24},{1,5},{5... | collective-permute-start | bytes 49160 | tf_op jit(solution)/shard_map/ppermute | solution.py:88
  53.1 10.7 %collective-permute-start.1 = (f32[32,128]{1,0:T(8,128)S(1)}, f32[32,128]{1,0:T(8,128)S(1)}, u32[]{:S(2)}, u32[]{:S(2)}) collective-permute-start(f32[32,128]{1,0:T(8,128)S(1)} %add.102), channel_id=1, source_target_pairs={{0,8},{4,12},{8,0},{12,4},{16,24},{20,28},{24,16},{28,20},{1,9},{5... | collective-permute-start | bytes 49160 | tf_op jit(solution)/shard_map/ppermute | solution.py:88
  63.8 3.8 %collective-permute-start.2 = (f32[32,128]{1,0:T(8,128)S(1)}, f32[32,128]{1,0:T(8,128)S(1)}, u32[]{:S(2)}, u32[]{:S(2)}) collective-permute-start(f32[32,128]{1,0:T(8,128)S(1)} %add.103), channel_id=1, source_target_pairs={{0,16},{4,20},{8,24},{12,28},{16,0},{20,4},{24,8},{28,12},{1,17},{... | collective-permute-start | bytes 49160 | tf_op jit(solution)/shard_map/ppermute | solution.py:88
  64.4 33.2 %copy-start.9 = (s32[24]{0:T(128)S(1)}, s32[24]{0:T(128)}, u32[]{:S(2)}) copy-start(s32[24]{0:T(128)} %param.21) | copy-start | bytes 292
  92.8 8.8 %all-to-all-start.2 = ((f32[8,27,128]{2,1,0:T(8,128)}), f32[8,27,128]{2,1,0:T(8,128)S(1)}, u32[]{:S(2)}, u32[]{:S(2)}) async-start(f32[8,27,128]{2,1,0:T(8,128)} %reshape.44), calls=%async_computation.3 | async-start | bytes 262144 | tf_op jit(solution)/shard_map/all_to_all | solution.py:63
  96.2 22.4 %reduce-scatter.6.cloned.1.call-start = ((), (), s32[]{:S(2)}) async-start(), calls=%async_computation.8 | async-start | bytes 81920 | tf_op jit(solution)/shard_map/reduce_scatter | solution.py:84
  118.6 9.9 %collective-permute-start.3 = (f32[32,128]{1,0:T(8,128)}, f32[32,128]{1,0:T(8,128)S(1)}, u32[]{:S(2)}, u32[]{:S(2)}) collective-permute-start(f32[32,128]{1,0:T(8,128)} %reduce-scatter.6.cloned.1.call-done), channel_id=1, source_target_pairs={{0,4},{4,0},{8,12},{12,8},{16,20},{20,16},{24,28},{28,24},{1,5},{5... | collective-permute-start | bytes 49160 | tf_op jit(solution)/shard_map/ppermute | solution.py:88
  129.2 10.7 %collective-permute-start.4 = (f32[32,128]{1,0:T(8,128)S(1)}, f32[32,128]{1,0:T(8,128)S(1)}, u32[]{:S(2)}, u32[]{:S(2)}) collective-permute-start(f32[32,128]{1,0:T(8,128)S(1)} %add.108), channel_id=1, source_target_pairs={{0,8},{4,12},{8,0},{12,4},{16,24},{20,28},{24,16},{28,20},{1,9},{5... | collective-permute-start | bytes 49160 | tf_op jit(solution)/shard_map/ppermute | solution.py:88
  139.9 3.8 %collective-permute-start.5 = (f32[32,128]{1,0:T(8,128)S(1)}, f32[32,128]{1,0:T(8,128)S(1)}, u32[]{:S(2)}, u32[]{:S(2)}) collective-permute-start(f32[32,128]{1,0:T(8,128)S(1)} %add.109), channel_id=1, source_target_pairs={{0,16},{4,20},{8,24},{12,28},{16,0},{20,4},{24,8},{28,12},{1,17},{... | collective-permute-start | bytes 49160 | tf_op jit(solution)/shard_map/ppermute | solution.py:88
  168.8 8.8 %all-to-all-start.3 = ((f32[8,27,128]{2,1,0:T(8,128)}), f32[8,27,128]{2,1,0:T(8,128)S(1)}, u32[]{:S(2)}, u32[]{:S(2)}) async-start(f32[8,27,128]{2,1,0:T(8,128)} %reshape.46), calls=%async_computation.5 | async-start | bytes 262144 | tf_op jit(solution)/shard_map/all_to_all | solution.py:63
  172.2 21.0 %reduce-scatter.8.cloned.1.call-start = ((), (), s32[]{:S(2)}) async-start(), calls=%async_computation.9 | async-start | bytes 81920 | tf_op jit(solution)/shard_map/reduce_scatter | solution.py:84
  193.2 9.9 %collective-permute-start.6 = (f32[32,128]{1,0:T(8,128)}, f32[32,128]{1,0:T(8,128)S(1)}, u32[]{:S(2)}, u32[]{:S(2)}) collective-permute-start(f32[32,128]{1,0:T(8,128)} %reduce-scatter.8.cloned.1.call-done), channel_id=1, source_target_pairs={{0,4},{4,0},{8,12},{12,8},{16,20},{20,16},{24,28},{28,24},{1,5},{5... | collective-permute-start | bytes 49160 | tf_op jit(solution)/shard_map/ppermute | solution.py:88
  203.8 10.6 %collective-permute-start.7 = (f32[32,128]{1,0:T(8,128)S(1)}, f32[32,128]{1,0:T(8,128)S(1)}, u32[]{:S(2)}, u32[]{:S(2)}) collective-permute-start(f32[32,128]{1,0:T(8,128)S(1)} %add.113), channel_id=1, source_target_pairs={{0,8},{4,12},{8,0},{12,4},{16,24},{20,28},{24,16},{28,20},{1,9},{5... | collective-permute-start | bytes 49160 | tf_op jit(solution)/shard_map/ppermute | solution.py:88
  214.4 3.8 %collective-permute-start.8 = (f32[32,128]{1,0:T(8,128)S(1)}, f32[32,128]{1,0:T(8,128)S(1)}, u32[]{:S(2)}, u32[]{:S(2)}) collective-permute-start(f32[32,128]{1,0:T(8,128)S(1)} %add.114), channel_id=1, source_target_pairs={{0,16},{4,20},{8,24},{12,28},{16,0},{20,4},{24,8},{28,12},{1,17},{... | collective-permute-start | bytes 49160 | tf_op jit(solution)/shard_map/ppermute | solution.py:88
Sparse Core Ops, SparseCore 0:
  21.5 20.9 reduce-scatter.3
  99.2 19.3 reduce-scatter.5
  175.2 17.9 reduce-scatter.7
